TPU v7x, 256 devices: a whole 4x4x8 slice. The times are simulated.
256 devices in a mesh: dp: 16 (over y, x), rows: 16 (over z, core).
Axes of the slice: x: 4, y: 4, z: 8, core: 2. Of those that a mesh axis runs over, the one named last changes fastest.
Arguments:
- grad_out: bfloat16 [8192, 4096], P('dp', 'rows'), may hold values from -0.375 to 0.375
- activations: bfloat16 [8192, 4096], P('dp', 'rows'), may hold values from -6 to 6
- error_feedback: float32 [16, 4096, 4096], P('dp', 'rows'), may hold values from -6 to 6
- momentum: bfloat16 [4096, 4096], P('rows'), may hold values from -1.1953125 to 1.1953125
- right_factor: float32 [4096, 128], P('rows'), may hold values from -0.09375 to 0.09375
Outputs:
- new_error: float32 [16, 4096, 4096], P('dp', 'rows')
- new_momentum: bfloat16 [4096, 4096], P('rows')
- new_right: float32 [4096, 128], P('rows')
All inputs are finite; a program needn't handle non-finite values.
Results may differ from a plain program's by a relative error of at most 0.0012.
Values may be sent and summed in bfloat16 or wider, within the bound.
A program may use at most 64 MiB of HBM per device.

v0:
```python
import jax
import jax.numpy as jnp
from jax import lax
from jax.sharding import PartitionSpec as P

PASSES = 2
MOMENTUM_RATE = 0.9
HIGHEST = lax.Precision.HIGHEST


def from_everyone(value, axis):
    copies = jnp.broadcast_to(value, (lax.axis_size(axis), *value.shape))
    return lax.all_to_all(copies, axis, split_axis=0, concat_axis=0, tiled=True)


def joined_along(tiles, dim):
    lengths = list(tiles.shape[1:])
    lengths[dim] *= tiles.shape[0]
    return jnp.moveaxis(tiles, 0, dim).reshape(lengths)


def gathered_copies(value, axis, dim):
    tiles = from_everyone(value, axis)
    return joined_along(tiles, dim)


def of_everyone(value, axis):
    everything = from_everyone(value, axis)
    return jnp.sum(everything, axis=0)


def total_of_pieces(value, axis):
    return lax.all_gather(value, axis).sum(0)


def cut_along(value, dim, count):
    lengths = value.shape
    tiles = value.reshape(*lengths[:dim], count, lengths[dim] // count, *lengths[dim + 1 :])
    return jnp.moveaxis(tiles, dim, 0)


def sent_and_summed(value, axis, dim):
    count = lax.axis_size(axis)
    tiles = lax.all_to_all(cut_along(value, dim, count), axis, 0, 0, tiled=True)
    return jnp.sum(tiles, axis=0)


def per_device(grad_out, activations, error_feedback, momentum, right_factor):
    replicas = lax.axis_size("dp")
    grad_local = lax.dot_general(
        grad_out,
        lax.all_gather(activations, "rows", axis=1, tiled=True),
        (((0,), (0,)), ((), ())),
        preferred_element_type=jnp.float32,
    )
    merged = grad_local + error_feedback[0]
    right_full = gathered_copies(right_factor, "rows", 0)
    left_factor = None
    own_rows = None
    for pass_index in range(PASSES):
        local_term = jnp.dot(
            merged, right_full, precision=HIGHEST, preferred_element_type=jnp.float32
        )
        left_factor = of_everyone(local_term, "dp") / replicas
        gram_local = jnp.dot(
            left_factor.T, left_factor, precision=HIGHEST, preferred_element_type=jnp.float32
        )
        gram_matrix = total_of_pieces(gram_local, "rows")
        cholesky_lower = jnp.linalg.cholesky(gram_matrix)
        left_factor = jax.scipy.linalg.solve_triangular(cholesky_lower, left_factor.T, lower=True).T
        right_term = lax.dot_general(
            merged,
            left_factor,
            (((0,), (0,)), ((), ())),
            precision=HIGHEST,
            preferred_element_type=jnp.float32,
        )
        own_rows = sent_and_summed(right_term, "rows", 0)
        own_rows = of_everyone(own_rows, "dp") / replicas
        right_full = gathered_copies(own_rows, "rows", 0)
    approx = jnp.dot(
        left_factor, right_full.T, precision=HIGHEST, preferred_element_type=jnp.float32
    )
    new_error = (merged - approx)[None]
    new_momentum = (MOMENTUM_RATE * momentum.astype(jnp.float32) + approx).astype(jnp.bfloat16)
    return (new_error, new_momentum, own_rows)


def solution(mesh):
    return jax.shard_map(
        per_device,
        mesh=mesh,
        in_specs=(
            P("dp", "rows"),
            P("dp", "rows"),
            P("dp", "rows", None),
            P("rows", None),
            P("rows", None),
        ),
        out_specs=(P("dp", "rows", None), P("rows", None), P("rows", None)),
        check_vma=False,
    )
```

profile of v0, /device:TPU:1, one launch (start us, length us, event | category | flops | bytes accessed | tf_op | source)
XLA Modules:
  0.0 616.3 jit_solution(16566047498738973250)
XLA Ops:
  7.2 0.7 all-gather.6.cloned.1.call-update
  7.9 2.4 broadcast_in_dim.25
  10.3 10.0 %all-to-all-start = ((f32[16,256,128]{2,1,0:T(8,128)}), f32[16,256,128]{2,1,0:T(8,128)S(1)}, u32[]{:S(2)}, u32[]{:S(2)}) async-start(f32[16,256,128]{2,1,0:T(8,128)} %broadcast_in_dim.25), calls=%async_computation | async-start | bytes 4194304 | tf_op jit(solution)/shard_map/all_to_all | solution.py:13
  20.4 75.3 %all-gather.6.cloned.1.call-done = bf16[512,4096]{1,0:T(8,128)(2,1)} async-done(((bf16[512,256]{1,0:T(8,128)(2,1)}), bf16[512,4096]{1,0:T(8,128)(2,1)}) %all-gather.6.cloned.1.call-update) | async-done | bytes 4194320 | tf_op jit(solution)/shard_map/all_gather | solution.py:52
  95.7 6.8 %convolution_add_fusion = f32[256,4096]{1,0:T(8,128)} fusion(bf16[512,256]{1,0:T(8,128)(2,1)S(1)} %copy-done, bf16[512,4096]{1,0:T(8,128)(2,1)} %all-gather.6.cloned.1.call-done, f32[1,256,4096]{2,1,0:T(8,128)} %param.10), kind=kOutput, calls=%fused_computation | convolution fusion | flops 1074790400 | bytes 12845056 | tf_op jit(solution)/shard_map/dot_general | solution.py:50
  102.5 5.9 fusion.26
  108.6 34.5 %all_to_all.45 = f32[16,256,128]{2,1,0:T(8,128)S(1)} all-to-all(f32[16,256,128]{2,1,0:T(8,128)S(1)} %broadcast_in_dim.26), channel_id=1, replica_groups=mesh['dp'=16,'rows'=16] {'dp'}, dimensions={0} | all-to-all | bytes 4194304 | tf_op jit(solution)/shard_map/all_to_all | solution.py:13
  143.2 1.0 fusion.8
  144.4 34.3 %all-gather.8.cloned.1.call-done = f32[2048,128]{1,0:T(8,128)} async-done(((f32[128,128]{1,0:T(8,128)}), f32[2048,128]{1,0:T(8,128)}) %all-gather.8.cloned.1.call-update) | async-done | bytes 1048592 | tf_op jit(solution)/shard_map/all_gather | solution.py:33
  178.7 1.3 reduce_sum.73
  180.1 11.7 %cholesky.44 = f32[128,128]{1,0:T(8,128)S(1)} custom-call(f32[128,128]{1,0:T(8,128)S(1)} %fusion.15), custom_call_target="Cholesky" | custom-call | tf_op jit(solution)/shard_map/jit(cholesky)/cholesky | solution.py:69
  191.9 0.6 compare_reduce_fusion.1
  192.5 0.7 fusion.10
  193.2 9.8 %custom-call.6 = f32[1,128,128]{1,2,0:T(8,128)S(1)} custom-call(f32[1,128,128]{2,1,0:T(8,128)S(1)} %fusion.10), custom_call_target="InvertDiagBlocksLowerTriangular" | custom-call | tf_op jit(solution)/shard_map/jit(_solve_triangular)/triangular_solve | solution.py:70
  203.3 8.7 %fusion.27 = f32[4096,128]{1,0:T(8,128)S(1)} fusion(f32[256,4096]{1,0:T(8,128)} %convolution_add_fusion, f32[128,256]{1,0:T(8,128)S(1)} %fusion.2), kind=kOutput, calls=%fused_computation.41 | convolution fusion | flops 1610612736 | bytes 6422528 | tf_op jit(solution)/shard_map/dot_general | solution.py:71
  212.0 55.3 %all_to_all.46 = f32[16,256,128]{2,1,0:T(8,128)S(1)} all-to-all(f32[16,256,128]{2,1,0:T(8,128)S(1)} %bitcast.49), channel_id=1, replica_groups=mesh['dp'=16,'rows'=16] {'rows'}, dimensions={0} | all-to-all | bytes 4194304 | tf_op jit(solution)/shard_map/all_to_all | solution.py:44
  267.6 34.7 %all_to_all.47 = f32[16,256,128]{2,1,0:T(8,128)S(1)} all-to-all(f32[16,256,128]{2,1,0:T(8,128)S(1)} %broadcast_in_dim.27), channel_id=1, replica_groups=mesh['dp'=16,'rows'=16] {'dp'}, dimensions={0} | all-to-all | bytes 4194304 | tf_op jit(solution)/shard_map/all_to_all | solution.py:13
  302.6 54.5 %all_to_all.48 = f32[16,256,128]{2,1,0:T(8,128)S(1)} all-to-all(f32[16,256,128]{2,1,0:T(8,128)S(1)} %broadcast_in_dim.28), channel_id=1, replica_groups=mesh['dp'=16,'rows'=16] {'rows'}, dimensions={0} | all-to-all | bytes 4194304 | tf_op jit(solution)/shard_map/all_to_all | solution.py:13
  357.1 3.5 fusion.28
  360.8 31.1 %all_to_all.49 = f32[16,256,128]{2,1,0:T(8,128)S(1)} all-to-all(f32[16,256,128]{2,1,0:T(8,128)S(1)} %broadcast_in_dim.29), channel_id=1, replica_groups=mesh['dp'=16,'rows'=16] {'dp'}, dimensions={0} | all-to-all | bytes 4194304 | tf_op jit(solution)/shard_map/all_to_all | solution.py:13
  392.0 1.0 fusion.5
  393.0 32.6 %all-gather.10.cloned.1.call-done = f32[2048,128]{1,0:T(8,128)} async-done(((f32[128,128]{1,0:T(8,128)}), f32[2048,128]{1,0:T(8,128)}) %all-gather.10.cloned.1.call-update) | async-done | bytes 1048592 | tf_op jit(solution)/shard_map/all_gather | solution.py:33
  425.6 1.3 reduce_sum.77
  427.0 11.7 %cholesky.55 = f32[128,128]{1,0:T(8,128)S(1)} custom-call(f32[128,128]{1,0:T(8,128)S(1)} %fusion.13), custom_call_target="Cholesky" | custom-call | tf_op jit(solution)/shard_map/jit(cholesky)/cholesky | solution.py:69
  438.7 0.6 compare_reduce_fusion
  439.4 0.7 fusion.11
  440.1 9.8 %custom-call.7 = f32[1,128,128]{1,2,0:T(8,128)S(1)} custom-call(f32[1,128,128]{2,1,0:T(8,128)S(1)} %fusion.11), custom_call_target="InvertDiagBlocksLowerTriangular" | custom-call | tf_op jit(solution)/shard_map/jit(_solve_triangular)/triangular_solve | solution.py:70
  450.2 8.7 %fusion.29 = f32[4096,128]{1,0:T(8,128)S(1)} fusion(f32[256,4096]{1,0:T(8,128)} %convolution_add_fusion, f32[128,256]{1,0:T(8,128)S(1)} %fusion), kind=kOutput, calls=%fused_computation.43 | convolution fusion | flops 1610612736 | bytes 6422528 | tf_op jit(solution)/shard_map/dot_general | solution.py:71
  458.8 55.3 %all_to_all.50 = f32[16,256,128]{2,1,0:T(8,128)S(1)} all-to-all(f32[16,256,128]{2,1,0:T(8,128)S(1)} %bitcast.51), channel_id=1, replica_groups=mesh['dp'=16,'rows'=16] {'rows'}, dimensions={0} | all-to-all | bytes 4194304 | tf_op jit(solution)/shard_map/all_to_all | solution.py:44
  514.4 34.7 %all_to_all.51 = f32[16,256,128]{2,1,0:T(8,128)S(1)} all-to-all(f32[16,256,128]{2,1,0:T(8,128)S(1)} %broadcast_in_dim.30), channel_id=1, replica_groups=mesh['dp'=16,'rows'=16] {'dp'}, dimensions={0} | all-to-all | bytes 4194304 | tf_op jit(solution)/shard_map/all_to_all | solution.py:13
  549.5 54.5 %all_to_all.52 = f32[16,256,128]{2,1,0:T(8,128)S(1)} all-to-all(f32[16,256,128]{2,1,0:T(8,128)S(1)} %broadcast_in_dim.31), channel_id=1, replica_groups=mesh['dp'=16,'rows'=16] {'rows'}, dimensions={0} | all-to-all | bytes 4194304 | tf_op jit(solution)/shard_map/all_to_all | solution.py:13
  604.0 5.8 add_convert_fusion
  (38 shorter events, 3.1 us)
Async XLA Ops:
  7.2 88.5 %copy-start = (bf16[512,256]{1,0:T(8,128)(2,1)S(1)}, bf16[512,256]{1,0:T(8,128)(2,1)}, u32[]{:S(2)}) copy-start(bf16[512,256]{1,0:T(8,128)(2,1)} %param.8) | copy-start | bytes 786436
  7.2 88.5 %all-gather.6.cloned.1.call-start = ((), (), s32[]{:S(2)}) async-start(), calls=%async_computation.9 | async-start | bytes 4456448 | tf_op jit(solution)/shard_map/all_gather | solution.py:52
  10.3 92.1 %all-to-all-start = ((f32[16,256,128]{2,1,0:T(8,128)}), f32[16,256,128]{2,1,0:T(8,128)S(1)}, u32[]{:S(2)}, u32[]{:S(2)}) async-start(f32[16,256,128]{2,1,0:T(8,128)} %broadcast_in_dim.25), calls=%async_computation | async-start | bytes 4194304 | tf_op jit(solution)/shard_map/all_to_all | solution.py:13
  20.3 158.4 %all-gather.8.cloned.1.call-start = ((), (), s32[]{:S(2)}) async-start(), calls=%async_computation.10 | async-start | bytes 1114112 | tf_op jit(solution)/shard_map/all_gather | solution.py:33
  144.2 281.4 %all-gather.10.cloned.1.call-start = ((), (), s32[]{:S(2)}) async-start(), calls=%async_computation.11 | async-start | bytes 1114112 | tf_op jit(solution)/shard_map/all_gather | solution.py:33
  302.6 54.6 %copy-start.1 = (f32[256,4096]{1,0:T(8,128)S(1)}, f32[256,4096]{1,0:T(8,128)}, u32[]{:S(2)}) copy-start(f32[256,4096]{1,0:T(8,128)} %convolution_add_fusion) | copy-start | bytes 12582916
  549.2 54.8 %copy-start.4 = (f32[256,128]{1,0:T(8,128)}, f32[256,128]{1,0:T(8,128)S(1)}, u32[]{:S(2)}) copy-start(f32[256,128]{1,0:T(8,128)S(1)} %broadcast_multiply_fusion) | copy-start | bytes 393220
  549.2 54.8 %copy-start.3 = (bf16[256,4096]{1,0:T(8,128)(2,1)S(1)}, bf16[256,4096]{1,0:T(8,128)(2,1)}, u32[]{:S(2)}) copy-start(bf16[256,4096]{1,0:T(8,128)(2,1)} %param.11) | copy-start | bytes 6291460
  549.5 54.6 %copy-start.2 = (f32[256,4096]{1,0:T(8,128)S(1)}, f32[256,4096]{1,0:T(8,128)}, u32[]{:S(2)}) copy-start(f32[256,4096]{1,0:T(8,128)} %convolution_add_fusion) | copy-start | bytes 12582916
Sparse Core Ops, SparseCore 0:
  9.7 85.8 all-gather.5
  144.3 34.3 all-gather.7
  393.1 32.4 all-gather.9
where the time goes:
time: 617 us; the launch traced here: 616 us
  blocking collectives  355 us (58%)
  waiting for transfers between devices  143 us (23%)
  other arithmetic  49 us (8%)
  matrix products  41.9 us (7%)
  between operations  14 us (2%)
  starting transfers between devices  10.3 us (2%)
    all_to_all x6, blocking collectives, from_everyone(): return lax.all_to_all(copies, axis, split_axis=0, concat_axis=0, tiled=True)  244 us
    all_to_all x2, blocking collectives, sent_and_summed(): tiles = lax.all_to_all(cut_along(value, dim, count), axis, 0, 0, tiled=True)  111 us
    all_gather x1, waiting for transfers between devices, per_device(): lax.all_gather(activations, 'rows', axis=1, tiled=True)  75.3 us
    all_gather x2, waiting for transfers between devices, total_of_pieces(): return lax.all_gather(value, axis).sum(0)  66.9 us
    another operation x6, other arithmetic, per_device(): cholesky_lower = jnp.linalg.cholesky(gram_matrix)  24.8 us
    another operation x4, other arithmetic, per_device(): jax.scipy.linalg.solve_triangular(cholesky_lower, left_factor.T, lower=True)  20.9 us
    dot_general x2, matrix products, per_device(): lax.dot_general(merged, left_factor, (((0,), (0,)), ((), ())), precision=...  17.3 us
  transfers between devices with their start and end apart: 4, of which 3 were waited for; matrix products, arithmetic and copies ran while one was open for 1% of the time, Pallas kernels for 0%

commit v1 on v0

--- a/solution.py
+++ b/solution.py
@@ -6,6 +6,11 @@
 PASSES = 2
 MOMENTUM_RATE = 0.9
 HIGHEST = lax.Precision.HIGHEST
+
+
+def gather_from_all(value, axis, dim):
+    copies = jnp.concatenate([value] * lax.axis_size(axis), axis=dim)
+    return lax.all_to_all(copies, axis, dim, dim, tiled=True)
 
 
 def from_everyone(value, axis):
@@ -49,7 +54,7 @@
     replicas = lax.axis_size("dp")
     grad_local = lax.dot_general(
         grad_out,
-        lax.all_gather(activations, "rows", axis=1, tiled=True),
+        gather_from_all(activations, "rows", 1),
         (((0,), (0,)), ((), ())),
         preferred_element_type=jnp.float32,
     )

time: 617 us -> 716 us (1.16)
  blocking collectives: 355 us -> 461 us
  waiting for transfers between devices: 143 us -> 97.1 us
  local copies, waits for them, and re-layouts: 3.81 us -> 36 us
    all_to_all x0 -> x1, blocking collectives: none -> 106 us  [gather_from_all(): return lax.all_to_all(copies, axis, dim, dim, tiled=True)]
    all_gather x1 -> x0, waiting for transfers between devices: 75.3 us -> none  [per_device(): lax.all_gather(activations, 'rows', axis=1, tiled=True)]
    all_to_all x1, waiting for transfers between devices: 0.01 us -> 29.6 us  [from_everyone(): return lax.all_to_all(copies, axis, split_axis=0, concat_axis=0, tiled=True)]
    unnamed x10 -> x32, local copies, waits for them, and re-layouts: 0.03 us -> 14.7 us
    all_to_all x0 -> x2, local copies, waits for them, and re-layouts: none -> 12.8 us  [gather_from_all(): return lax.all_to_all(copies, axis, dim, dim, tiled=True)]
  transfers between devices with their start and end apart: 4 -> 3, of which waited for: 3 -> 3; matrix products, arithmetic and copies ran while one was open for 1% -> 3% of each run, Pallas kernels for 0% -> 0%
where the time goes in v1:
time: 716 us; the launch traced here: 709 us
  blocking collectives  461 us (64%)
  waiting for transfers between devices  97.1 us (14%)
  other arithmetic  55 us (8%)
  matrix products  41 us (6%)
  local copies, waits for them, and re-layouts  36 us (5%)
  between operations  14.6 us (2%)
    all_to_all x6, blocking collectives, from_everyone(): return lax.all_to_all(copies, axis, split_axis=0, concat_axis=0, tiled=True)  244 us
    all_to_all x2, blocking collectives, sent_and_summed(): tiles = lax.all_to_all(cut_along(value, dim, count), axis, 0, 0, tiled=True)  111 us
    all_to_all x1, blocking collectives, gather_from_all(): return lax.all_to_all(copies, axis, dim, dim, tiled=True)  106 us
    all_gather x2, waiting for transfers between devices, total_of_pieces(): return lax.all_gather(value, axis).sum(0)  67.5 us
    all_to_all x1, waiting for transfers between devices, from_everyone(): return lax.all_to_all(copies, axis, split_axis=0, concat_axis=0, tiled=True)  29.6 us
    another operation x6, other arithmetic, per_device(): cholesky_lower = jnp.linalg.cholesky(gram_matrix)  24.8 us
    another operation x4, other arithmetic, per_device(): jax.scipy.linalg.solve_triangular(cholesky_lower, left_factor.T, lower=True)  20.9 us
    dot_general x2, matrix products, per_device(): jnp.dot(merged, right_full, precision=HIGHEST, preferred_element_type=jnp...  15.3 us
  transfers between devices with their start and end apart: 3, of which 3 were waited for; matrix products, arithmetic and copies ran while one was open for 3% of the time, Pallas kernels for 0%

profile of v1, /device:TPU:1, one launch (start us, length us, event | category | flops | bytes accessed | tf_op | source)
XLA Modules:
  0.0 708.7 jit_solution(18333990449300950790)
XLA Ops:
  8.8 2.0 copy-done.3
  10.8 6.4 copy.57
  17.2 106.1 %all_to_all.57 = bf16[512,16,256]{2,0,1:T(8,128)(2,1)} all-to-all(bf16[512,16,256]{2,0,1:T(8,128)(2,1)} %copy.57), channel_id=1, replica_groups=mesh['dp'=16,'rows'=16] {'rows'}, dimensions={1} | all-to-all | bytes 8388608 | tf_op jit(solution)/shard_map/all_to_all | solution.py:13
  123.2 1.5 broadcast_in_dim.25
  124.7 3.6 all-to-all-start.1
  128.4 5.6 copy.59
  134.0 6.4 copy.58
  140.4 6.7 fusion
  147.1 29.6 %all-to-all-done.1 = f32[16,256,128]{2,1,0:T(8,128)S(1)} async-done(((f32[16,256,128]{2,1,0:T(8,128)}), f32[16,256,128]{2,1,0:T(8,128)S(1)}, u32[]{:S(2)}, u32[]{:S(2)}) %all-to-all-start.1) | async-done | bytes 2097184 | tf_op jit(solution)/shard_map/all_to_all | solution.py:18
  176.7 8.5 %fusion.27 = f32[256,128]{1,0:T(8,128)S(1)} fusion(f32[256,4096]{0,1:T(8,128)} %fusion, f32[4096,128]{1,0:T(8,128)S(1)} %bitcast.54), kind=kOutput, calls=%fused_computation.57 | convolution fusion | flops 1610612736 | bytes 6422528 | tf_op jit(solution)/shard_map/dot_general | solution.py:66
  185.4 34.2 %all_to_all.58 = f32[16,256,128]{2,1,0:T(8,128)S(1)} all-to-all(f32[16,256,128]{2,1,0:T(8,128)S(1)} %broadcast_in_dim.26), channel_id=1, replica_groups=mesh['dp'=16,'rows'=16] {'dp'}, dimensions={0} | all-to-all | bytes 4194304 | tf_op jit(solution)/shard_map/all_to_all | solution.py:18
  221.2 34.9 %all-gather.5.cloned.1.call-done = f32[2048,128]{1,0:T(8,128)} async-done(((f32[128,128]{1,0:T(8,128)}), f32[2048,128]{1,0:T(8,128)}) %all-gather.5.cloned.1.call-update) | async-done | bytes 1048592 | tf_op jit(solution)/shard_map/all_gather | solution.py:38
  256.0 1.3 reduce_sum.73
  257.4 11.7 %cholesky.44 = f32[128,128]{1,0:T(8,128)S(1)} custom-call(f32[128,128]{1,0:T(8,128)S(1)} %fusion.16), custom_call_target="Cholesky" | custom-call | tf_op jit(solution)/shard_map/jit(cholesky)/cholesky | solution.py:74
  270.5 9.8 %custom-call.6 = f32[1,128,128]{1,2,0:T(8,128)S(1)} custom-call(f32[1,128,128]{2,1,0:T(8,128)S(1)} %fusion.11), custom_call_target="InvertDiagBlocksLowerTriangular" | custom-call | tf_op jit(solution)/shard_map/jit(_solve_triangular)/triangular_solve | solution.py:75
  280.6 5.3 fusion.28
  285.9 55.3 %all_to_all.59 = f32[16,256,128]{2,1,0:T(8,128)S(1)} all-to-all(f32[16,256,128]{2,1,0:T(8,128)S(1)} %bitcast.55), channel_id=1, replica_groups=mesh['dp'=16,'rows'=16] {'rows'}, dimensions={0} | all-to-all | bytes 4194304 | tf_op jit(solution)/shard_map/all_to_all | solution.py:49
  341.5 34.7 %all_to_all.60 = f32[16,256,128]{2,1,0:T(8,128)S(1)} all-to-all(f32[16,256,128]{2,1,0:T(8,128)S(1)} %broadcast_in_dim.27), channel_id=1, replica_groups=mesh['dp'=16,'rows'=16] {'dp'}, dimensions={0} | all-to-all | bytes 4194304 | tf_op jit(solution)/shard_map/all_to_all | solution.py:18
  376.5 55.1 %all_to_all.61 = f32[16,256,128]{2,1,0:T(8,128)S(1)} all-to-all(f32[16,256,128]{2,1,0:T(8,128)S(1)} %broadcast_in_dim.28), channel_id=1, replica_groups=mesh['dp'=16,'rows'=16] {'rows'}, dimensions={0} | all-to-all | bytes 4194304 | tf_op jit(solution)/shard_map/all_to_all | solution.py:18
  431.6 6.8 fusion.29
  438.6 31.2 %all_to_all.62 = f32[16,256,128]{2,1,0:T(8,128)S(1)} all-to-all(f32[16,256,128]{2,1,0:T(8,128)S(1)} %broadcast_in_dim.29), channel_id=1, replica_groups=mesh['dp'=16,'rows'=16] {'dp'}, dimensions={0} | all-to-all | bytes 4194304 | tf_op jit(solution)/shard_map/all_to_all | solution.py:18
  471.0 32.6 %all-gather.7.cloned.1.call-done = f32[2048,128]{1,0:T(8,128)} async-done(((f32[128,128]{1,0:T(8,128)}), f32[2048,128]{1,0:T(8,128)}) %all-gather.7.cloned.1.call-update) | async-done | bytes 1048592 | tf_op jit(solution)/shard_map/all_gather | solution.py:38
  505.0 11.7 %cholesky.55 = f32[128,128]{1,0:T(8,128)S(1)} custom-call(f32[128,128]{1,0:T(8,128)S(1)} %fusion.14), custom_call_target="Cholesky" | custom-call | tf_op jit(solution)/shard_map/jit(cholesky)/cholesky | solution.py:74
  518.0 9.8 %custom-call.7 = f32[1,128,128]{1,2,0:T(8,128)S(1)} custom-call(f32[1,128,128]{2,1,0:T(8,128)S(1)} %fusion.12), custom_call_target="InvertDiagBlocksLowerTriangular" | custom-call | tf_op jit(solution)/shard_map/jit(_solve_triangular)/triangular_solve | solution.py:75
  528.2 5.3 fusion.30
  533.5 55.3 %all_to_all.63 = f32[16,256,128]{2,1,0:T(8,128)S(1)} all-to-all(f32[16,256,128]{2,1,0:T(8,128)S(1)} %bitcast.57), channel_id=1, replica_groups=mesh['dp'=16,'rows'=16] {'rows'}, dimensions={0} | all-to-all | bytes 4194304 | tf_op jit(solution)/shard_map/all_to_all | solution.py:49
  589.1 34.7 %all_to_all.64 = f32[16,256,128]{2,1,0:T(8,128)S(1)} all-to-all(f32[16,256,128]{2,1,0:T(8,128)S(1)} %broadcast_in_dim.30), channel_id=1, replica_groups=mesh['dp'=16,'rows'=16] {'dp'}, dimensions={0} | all-to-all | bytes 4194304 | tf_op jit(solution)/shard_map/all_to_all | solution.py:18
  624.1 54.6 %all_to_all.65 = f32[16,256,128]{2,1,0:T(8,128)S(1)} all-to-all(f32[16,256,128]{2,1,0:T(8,128)S(1)} %broadcast_in_dim.31), channel_id=1, replica_groups=mesh['dp'=16,'rows'=16] {'rows'}, dimensions={0} | all-to-all | bytes 4194304 | tf_op jit(solution)/shard_map/all_to_all | solution.py:18
  678.7 5.7 add_convert_fusion
  684.4 5.6 copy.62
  690.0 6.0 subtract_bitcast_fusion
  696.0 5.6 copy.63
  (63 shorter events, 10.5 us)
Async XLA Ops:
  7.2 133.3 %copy-start = (bf16[512,256]{1,0:T(8,128)(2,1)S(1)}, bf16[512,256]{1,0:T(8,128)(2,1)}, u32[]{:S(2)}) copy-start(bf16[512,256]{1,0:T(8,128)(2,1)} %param.8) | copy-start | bytes 786436
  8.8 2.0 copy-start.3
  17.2 106.1 %copy-start.6 = (f32[256,128]{1,0:T(8,128)S(1)}, f32[256,128]{1,0:T(8,128)}, u32[]{:S(2)}) copy-start(f32[256,128]{1,0:T(8,128)} %param.12) | copy-start | bytes 393220
  124.7 52.0 %all-to-all-start.1 = ((f32[16,256,128]{2,1,0:T(8,128)}), f32[16,256,128]{2,1,0:T(8,128)S(1)}, u32[]{:S(2)}, u32[]{:S(2)}) async-start(f32[16,256,128]{2,1,0:T(8,128)} %broadcast_in_dim.25), calls=%async_computation.1 | async-start | bytes 4194304 | tf_op jit(solution)/shard_map/all_to_all | solution.py:18
  128.4 127.7 %all-gather.5.cloned.1.call-start = ((), (), s32[]{:S(2)}) async-start(), calls=%async_computation.10 | async-start | bytes 1114112 | tf_op jit(solution)/shard_map/all_gather | solution.py:38
  220.8 282.7 %all-gather.7.cloned.1.call-start = ((), (), s32[]{:S(2)}) async-start(), calls=%async_computation.11 | async-start | bytes 1114112 | tf_op jit(solution)/shard_map/all_gather | solution.py:38
  376.3 55.3 %copy-start.2 = (f32[256,4096]{0,1:T(8,128)S(1)}, f32[256,4096]{0,1:T(8,128)}, u32[]{:S(2)}) copy-start(f32[256,4096]{0,1:T(8,128)} %fusion) | copy-start | bytes 12582916
  623.8 54.9 %copy-start.4 = (bf16[256,4096]{1,0:T(8,128)(2,1)S(1)}, bf16[256,4096]{1,0:T(8,128)(2,1)}, u32[]{:S(2)}) copy-start(bf16[256,4096]{1,0:T(8,128)(2,1)} %param.11) | copy-start | bytes 6291460
  623.9 60.5 %copy-start.5 = (f32[256,128]{1,0:T(8,128)}, f32[256,128]{1,0:T(8,128)S(1)}, u32[]{:S(2)}) copy-start(f32[256,128]{1,0:T(8,128)S(1)} %broadcast_multiply_fusion) | copy-start | bytes 393220
  690.0 11.6 %copy-start.1 = (bf16[512,256]{1,0:T(8,128)(2,1)S(1)}, bf16[512,256]{1,0:T(8,128)(2,1)}, u32[]{:S(2)}) copy-start(bf16[512,256]{1,0:T(8,128)(2,1)} %param.8) | copy-start | bytes 786436
Sparse Core Ops, SparseCore 0:
  221.0 35.0 all-gather.4
  471.1 32.4 all-gather.6
